TPU v7x, 32 devices: a whole 2x2x4 slice. The times are simulated.
32 devices in a mesh: ga: 8 (over z, y), ba: 4 (over x, core).
Axes of the slice: x: 2, y: 2, z: 4, core: 2. Of those that a mesh axis runs over, the one named last changes fastest.
Arguments:
- coefficients: bfloat16 [10240, 6144], P('ga', 'ba')
- rotation: bfloat16 [6144, 6144], P('ga', 'ba'), may hold values from -0.078125 to 0.078125
Outputs:
- new_coefficients: bfloat16 [10240, 6144], P('ga', 'ba')
- band_rms: float32 [6144], P('ba')
All inputs are finite; a program needn't handle non-finite values.
Results may differ from a plain program's by a relative error of at most 0.0004.
Values may be sent and summed in bfloat16 or wider, within the bound.
A program may use at most 128 MiB of HBM per device.

v0:
```python
import jax
import jax.numpy as jnp
from jax import lax
from jax.sharding import PartitionSpec as P


def body(coefficients, rotation):
    all_bands = lax.all_gather(coefficients, "ba", axis=1, tiled=True)
    rotated = jnp.dot(
        all_bands,
        lax.all_gather(rotation, "ga", axis=0, tiled=True),
        preferred_element_type=jnp.float32,
    )
    squares = lax.psum(jnp.sum(rotated * rotated, axis=0), "ga")
    total_rows = coefficients.shape[0] * lax.axis_size("ga")
    band_rms = jnp.sqrt(squares / total_rows + 1e-06)
    return ((rotated / band_rms).astype(jnp.bfloat16), band_rms)


def solution(mesh):
    in_specs = (P("ga", "ba"), P("ga", "ba"))
    out_specs = (P("ga", "ba"), P("ba"))
    return jax.shard_map(body, mesh=mesh, in_specs=in_specs, out_specs=out_specs, check_vma=False)
```

profile of v0, /device:TPU:0, one launch (start us, length us, event | category | flops | bytes accessed | tf_op | source)
XLA Modules:
  0.0 543.6 jit_solution(14183646409815637874)
XLA Ops:
  7.2 0.0 all-gather.3.cloned.1.call-start
  7.2 0.7 all-gather.3.cloned.1.call-update
  7.9 0.0 all-gather.5.cloned.1.call-start
  7.9 0.7 all-gather.5.cloned.1.call-update
  8.6 103.6 %all-gather.3.cloned.1.call-done = bf16[1280,6144]{1,0:T(8,128)(2,1)} async-done(((bf16[1280,1536]{1,0:T(8,128)(2,1)}), bf16[1280,6144]{1,0:T(8,128)(2,1)}) %all-gather.3.cloned.1.call-update) | async-done | bytes 15728656 | tf_op jit(solution)/shard_map/all_gather | solution.py:8
  112.2 364.0 %all-gather.5.cloned.1.call-done = bf16[6144,1536]{1,0:T(8,128)(2,1)} async-done(((bf16[768,1536]{1,0:T(8,128)(2,1)}), bf16[6144,1536]{1,0:T(8,128)(2,1)}) %all-gather.5.cloned.1.call-update) | async-done | bytes 18874384 | tf_op jit(solution)/shard_map/all_gather | solution.py:11
  476.2 33.9 %multiply_reduce_fusion = (f32[1536]{0:T(1024)S(1)}, f32[1280,1536]{1,0:T(8,128)}) fusion(bf16[1280,6144]{1,0:T(8,128)(2,1)} %all-gather.3.cloned.1.call-done, bf16[6144,1536]{1,0:T(8,128)(2,1)} %all-gather.5.cloned.1.call-done), kind=kOutput, calls=%fused_computation.1 | convolution fusion | flops 24163121152 | bytes 42473472 | tf_op jit(solution)/shard_map/dot_general | solution.py:9
  510.1 20.4 %psum.7 = f32[1536]{0:T(1024)S(1)} all-reduce(f32[1536]{0:T(1024)S(1)} %get-tuple-element.2), channel_id=1, replica_groups=mesh['ga'=8,'ba'=4] {'ga'}, use_global_device_ids=true, to_apply=%region_1.0 | all-reduce | flops 1536 | bytes 12288 | tf_op jit(solution)/shard_map/psum | solution.py:14
  530.6 0.0 copy-start
  530.6 6.2 %divide_convert_fusion = bf16[1280,1536]{1,0:T(8,128)(2,1)} fusion(f32[1280,1536]{1,0:T(8,128)} %get-tuple-element.3, f32[1536]{0:T(1024)S(1)} %add_sqrt_fusion), kind=kLoop, calls=%fused_computation | loop fusion | flops 3932160 | bytes 11802624 | tf_op jit(solution)/shard_map/convert_element_type | solution.py:17
  536.8 0.0 copy-done
  (1 shorter events, 0.0 us)
Async XLA Ops:
  7.2 105.1 %all-gather.3.cloned.1.call-start = ((), (), s32[]{:S(2)}) async-start(), calls=%async_computation | async-start | bytes 19660800 | tf_op jit(solution)/shard_map/all_gather | solution.py:8
  7.9 468.3 %all-gather.5.cloned.1.call-start = ((), (), s32[]{:S(2)}) async-start(), calls=%async_computation.1 | async-start | bytes 21233664 | tf_op jit(solution)/shard_map/all_gather | solution.py:11
  530.6 6.2 %copy-start = (f32[1536]{0:T(1024)}, f32[1536]{0:T(1024)S(1)}, u32[]{:S(2)}) copy-start(f32[1536]{0:T(1024)S(1)} %add_sqrt_fusion) | copy-start | bytes 18436
Sparse Core Ops, SparseCore 0:
  9.5 102.6 all-gather.2
  113.8 362.3 all-gather.4
where the time goes:
time: 544 us
  waiting for transfers between devices  469 us (86%)
  matrix products  33.9 us (6%)
  blocking collectives  20.4 us (4%)
  between operations  14.1 us (3%)
  other arithmetic  6.19 us (1%)
    all_gather x1, waiting for transfers between devices, body(): lax.all_gather(rotation, 'ga', axis=0, tiled=True)  364 us
    all_gather x1, waiting for transfers between devices, body(): all_bands = lax.all_gather(coefficients, 'ba', axis=1, tiled=True)  104 us
    dot_general x1, matrix products, body(): jnp.dot(all_bands, lax.all_gather(rotation, 'ga', axis=0, tiled=True), pr...  33.9 us
    psum x1, blocking collectives, body(): squares = lax.psum(jnp.sum(rotated * rotated, axis=0), 'ga')  20.4 us
  transfers between devices with their start and end apart: 2, of which 2 were waited for; matrix products, arithmetic and copies ran while one was open for 0% of the time, Pallas kernels for 0%

commit v1 on v0

--- a/solution.py
+++ b/solution.py
@@ -5,7 +5,9 @@
 
 
 def body(coefficients, rotation):
-    all_bands = lax.all_gather(coefficients, "ba", axis=1, tiled=True)
+    all_bands = jnp.concatenate(
+        lax.all_to_all(jnp.stack([coefficients] * lax.axis_size("ba")), "ba", 0, 0), axis=1
+    )
     rotated = jnp.dot(
         all_bands,
         lax.all_gather(rotation, "ga", axis=0, tiled=True),

time: 544 us -> 443 us (0.81)
  waiting for transfers between devices: 469 us -> 181 us
  blocking collectives: 20.4 us -> 197 us
  local copies, waits for them, and re-layouts: 0.01 us -> 10 us
    all_gather x1, waiting for transfers between devices: 364 us -> 180 us  [body(): lax.all_gather(rotation, 'ga', axis=0, tiled=True)]
    all_to_all x0 -> x1, blocking collectives: none -> 177 us  [body(): lax.all_to_all(jnp.stack([coefficients] * lax.axis_size('ba')), 'ba', 0, 0)]
    all_gather x1 -> x0, waiting for transfers between devices: 104 us -> none  [body(): all_bands = lax.all_gather(coefficients, 'ba', axis=1, tiled=True)]
    unnamed x2 -> x3, local copies, waits for them, and re-layouts: 0.01 us -> 6.27 us
  transfers between devices with their start and end apart: 2 -> 1, of which waited for: 2 -> 1; matrix products, arithmetic and copies ran while one was open for 0% -> 2% of each run, Pallas kernels for 0% -> 0%
where the time goes in v1:
time: 443 us; the launch traced here: 442 us
  blocking collectives  197 us (44%)
  waiting for transfers between devices  181 us (41%)
  matrix products  34 us (8%)
  between operations  14.1 us (3%)
  local copies, waits for them, and re-layouts  10 us (2%)
  other arithmetic  6.19 us (1%)
    all_gather x1, waiting for transfers between devices, body(): lax.all_gather(rotation, 'ga', axis=0, tiled=True)  180 us
    all_to_all x1, blocking collectives, body(): lax.all_to_all(jnp.stack([coefficients] * lax.axis_size('ba')), 'ba', 0, 0)  177 us
    dot_general x1, matrix products, body(): jnp.dot(all_bands, lax.all_gather(rotation, 'ga', axis=0, tiled=True), pr...  34 us
    psum x1, blocking collectives, body(): squares = lax.psum(jnp.sum(rotated * rotated, axis=0), 'ga')  20.4 us
  transfers between devices with their start and end apart: 1, of which 1 were waited for; matrix products, arithmetic and copies ran while one was open for 2% of the time, Pallas kernels for 0%

profile of v1, /device:TPU:0, one launch (start us, length us, event | category | flops | bytes accessed | tf_op | source)
XLA Modules:
  0.0 442.2 jit_solution(4590798612077796172)
XLA Ops:
  7.2 0.0 all-gather.2.cloned.1.call-start
  7.2 0.7 all-gather.2.cloned.1.call-update
  7.9 6.3 %copy.4 = bf16[1280,1536]{0,1:T(8,128)(2,1)} copy(bf16[1280,1536]{1,0:T(8,128)(2,1)} %param.2) | data formatting | bytes 7864320 | tf_op args[0]
  14.2 3.8 stack.2
  17.9 176.8 %all_to_all.5 = bf16[4,1280,1536]{1,2,0:T(8,128)(2,1)} all-to-all(bf16[4,1280,1536]{1,2,0:T(8,128)(2,1)S(1)} %stack.2), channel_id=1, replica_groups=mesh['ga'=8,'ba'=4] {'ba'}, dimensions={0} | all-to-all | bytes 31457280 | tf_op jit(solution)/shard_map/all_to_all | solution.py:9
  194.7 179.9 %all-gather.2.cloned.1.call-done = bf16[6144,1536]{1,0:T(8,128)(2,1)} async-done(((bf16[768,1536]{1,0:T(8,128)(2,1)}), bf16[6144,1536]{1,0:T(8,128)(2,1)}) %all-gather.2.cloned.1.call-update) | async-done | bytes 18874384 | tf_op jit(solution)/shard_map/all_gather | solution.py:13
  374.7 34.0 %multiply_reduce_fusion = (f32[1536]{0:T(1024)S(1)}, f32[1280,1536]{1,0:T(8,128)}) fusion(bf16[1280,6144]{0,1:T(8,128)(2,1)} %bitcast.5, bf16[6144,1536]{1,0:T(8,128)(2,1)} %all-gather.2.cloned.1.call-done), kind=kOutput, calls=%fused_computation.1 | convolution fusion | flops 24163121152 | bytes 42473472 | tf_op jit(solution)/shard_map/dot_general | solution.py:11
  408.7 20.4 %psum.7 = f32[1536]{0:T(1024)S(1)} all-reduce(f32[1536]{0:T(1024)S(1)} %get-tuple-element.2), channel_id=1, replica_groups=mesh['ga'=8,'ba'=4] {'ga'}, use_global_device_ids=true, to_apply=%region_1.0 | all-reduce | flops 1536 | bytes 12288 | tf_op jit(solution)/shard_map/psum | solution.py:16
  429.2 0.0 copy-start
  429.2 6.2 %divide_convert_fusion = bf16[1280,1536]{1,0:T(8,128)(2,1)} fusion(f32[1280,1536]{1,0:T(8,128)} %get-tuple-element.3, f32[1536]{0:T(1024)S(1)} %add_sqrt_fusion), kind=kLoop, calls=%fused_computation | loop fusion | flops 3932160 | bytes 11802624 | tf_op jit(solution)/shard_map/convert_element_type | solution.py:19
  435.3 0.0 copy-done
  (1 shorter events, 0.0 us)
Async XLA Ops:
  7.2 367.5 %all-gather.2.cloned.1.call-start = ((), (), s32[]{:S(2)}) async-start(), calls=%async_computation.1 | async-start | bytes 21233664 | tf_op jit(solution)/shard_map/all_gather | solution.py:13
  429.2 6.2 %copy-start = (f32[1536]{0:T(1024)}, f32[1536]{0:T(1024)S(1)}, u32[]{:S(2)}) copy-start(f32[1536]{0:T(1024)S(1)} %add_sqrt_fusion) | copy-start | bytes 18436
Sparse Core Ops, SparseCore 0:
  9.5 365.1 all-gather.1
